TPU v7x, 32 devices: a whole 2x2x4 slice. The times are simulated.
32 devices in a mesh: row: 8 (over y, x, core), col: 4 (over z).
Axes of the slice: x: 2, y: 2, z: 4, core: 2. Of those that a mesh axis runs over, the one named last changes fastest.
Arguments:
- vectors: float32 [32768, 4096], P('row', 'col'), may hold values from -6 to 6
- reflectors: float32 [8, 32768, 128], P('col', 'row'), may hold values from -0.03125 to 0.03125
- triangles: float32 [8, 128, 128], P('col'), may hold values from -0.25 to 1.8, as said below
Outputs:
- transformed: float32 [32768, 4096], P('row', 'col')
Inputs may be any that keep to these rules, and one draw needn't show every extreme that they name: Each triangles[p] is upper triangular with diagonal entries between 0.5 and 1.8.
All inputs are finite; a program needn't handle non-finite values.
Results may differ from a plain program's by a relative error of at most 0.00013.
Values sent between devices are 32-bit elements; how exact they have to be, the bound alone decides.
A program may use at most 128 MiB of HBM per device.

v0:
```python
import jax
import jax.numpy as jnp
from jax import lax
from jax.sharding import PartitionSpec as P


def spread(block, axis, owner):
    block = jnp.where(lax.axis_index(axis) == owner, block, jnp.zeros_like(block))
    return lax.psum(block, axis)


def product_t(left, right):
    return lax.dot_general(
        left,
        right,
        (((0,), (0,)), ((), ())),
        precision=lax.Precision.HIGHEST,
        preferred_element_type=jnp.float32,
    )


def matmul(left, right):
    return jnp.dot(left, right, precision=lax.Precision.HIGHEST, preferred_element_type=jnp.float32)


def shards(vectors, reflectors, triangles):
    per_dev = reflectors.shape[0]
    panels = per_dev * lax.axis_size("col")

    def fetch(panel):
        local = panel % per_dev
        return (
            spread(reflectors[local], "col", panel // per_dev),
            spread(triangles[local], "col", panel // per_dev),
        )

    block = vectors
    for pair in range(panels // 2 - 1, -1, -1):
        basis_a, tri_a = fetch(2 * pair)
        basis_b, tri_b = fetch(2 * pair + 1)
        joined = jnp.concatenate([basis_a, basis_b], axis=1)
        summed, inner = lax.psum((product_t(joined, block), product_t(basis_a, basis_b)), "row")
        width = basis_a.shape[1]
        upper_w = summed[:width]
        lower_w = summed[width:]
        coupling = -matmul(matmul(tri_a, inner), tri_b)
        scaled_a = matmul(tri_a, upper_w) + matmul(coupling, lower_w)
        scaled_b = matmul(tri_b, lower_w)
        block = block - matmul(joined, jnp.concatenate([scaled_a, scaled_b], axis=0))
    return block


def solution(mesh):
    placed = (P("row", "col"), P("col", "row", None), P("col", None, None))
    return jax.shard_map(
        shards, mesh=mesh, in_specs=placed, out_specs=P("row", "col"), check_vma=False
    )
```

profile of v0, /device:TPU:0, one launch (start us, length us, event | category | flops | bytes accessed | tf_op | source)
XLA Modules:
  0.0 1032.6 jit_solution(5668326063415492051)
XLA Ops:
  6.5 0.0 all-reduce.19.cloned.1.call-start
  6.5 1.7 select_bitcast_fusion.9
  8.2 8.2 select_bitcast_fusion
  16.4 0.0 all-reduce.19.cloned.1.call-update
  16.4 0.0 all-reduce.17.cloned.1.call-start
  16.5 582.0 %all-reduce.19.cloned.1.call-done = (f32[4096,128]{1,0:T(8,128)}, f32[4096,128]{1,0:T(8,128)}, f32[128,128]{1,0:T(8,128)}, f32[128,128]{1,0:T(8,128)}, f32[4096,...) async-done(((f32[4096,128]{1,0:T(8,128)}, ...) | async-done | bytes 17301520 | tf_op jit(solution)/shard_map/psum | solution.py:9
  598.5 1.9 constant_dynamic-update-slice_fusion.1
  600.4 0.3 copy-done.8
  600.7 0.6 copy-done.9
  601.3 4.2 fusion.37
  605.6 0.0 copy-done.3
  605.6 1.5 constant_dynamic-update-slice_fusion.7
  607.1 1.5 constant_dynamic-update-slice_fusion.5
  608.6 1.5 constant_dynamic-update-slice_fusion.3
  610.2 0.2 constant_dynamic-update-slice_fusion
  610.3 0.0 copy-start
  610.3 2.0 copy-done
  612.4 30.1 %fusion.36 = f32[256,1024]{1,0:T(8,128)} fusion(f32[4096,256]{1,0:T(8,128)S(1)} %constant_dynamic-update-slice_fusion, f32[4096,1024]{1,0:T(8,128)} %param.3), kind=kOutput, calls=%fused_computation.72 | convolution fusion | flops 12884901888 | bytes 22020096 | tf_op jit(solution)/shard_map/dot_general | solution.py:13
  642.5 0.0 all-reduce.17.cloned.1.call-update
  642.5 0.3 all-reduce.15.cloned.1.call-start
  642.8 5.7 fusion.40
  648.5 1.5 constant_dynamic-update-slice_fusion.2
  650.0 48.5 %all-reduce.17.cloned.1.call-done = (f32[256,1024]{1,0:T(8,128)}, f32[128,128]{1,0:T(8,128)}) async-done(((f32[256,1024]{1,0:T(8,128)}, f32[128,128]{1,0:T(8,128)}), (f32[256,1024]{1,0:T(8,128)}, f32[128,128]{1,0:T(8,128)})) %all-reduce.17.cloned.1.call-update) | async-done | bytes 1114128 | tf_op jit(solution)/shard_map/psum | solution.py:42
  698.5 0.0 copy-done.17
  698.5 1.2 fusion.38
  699.7 1.7 fusion.18
  701.5 1.6 fusion.29
  703.1 0.2 convolution_negate_fusion.3
  703.3 1.6 convolution_add_fusion.3
  704.9 18.7 %convolution_subtract_fusion.3 = f32[4096,1024]{1,0:T(8,128)} fusion(f32[4096,1024]{1,0:T(8,128)} %param.3, f32[4096,256]{1,0:T(8,128)S(1)} %copy-done.1, f32[128,1024]{1,0:T(8,128)S(1)} %fusion.29, f32[128,1024]{1,0:T(8,128)S(1)} %convolution_add_fusion.3), kind=kOutput, calls=%fused_computation.3 | convolution fusion | flops 12889358336 | bytes 38797312 | tf_op jit(solution)/shard_map/dot_general | solution.py:23
  723.7 18.1 %fusion.39 = f32[256,1024]{1,0:T(8,128)} fusion(f32[4096,256]{1,0:T(8,128)} %constant_dynamic-update-slice_fusion.2, f32[4096,1024]{1,0:T(8,128)} %convolution_subtract_fusion.3), kind=kOutput, calls=%fused_computation.75 | convolution fusion | flops 12884901888 | bytes 22020096 | tf_op jit(solution)/shard_map/dot_general | solution.py:13
  741.8 0.0 all-reduce.15.cloned.1.call-update
  741.8 0.5 all-reduce.13.cloned.1.call-start
  742.4 5.7 fusion.43
  748.1 1.5 constant_dynamic-update-slice_fusion.4
  749.6 48.8 %all-reduce.15.cloned.1.call-done = (f32[256,1024]{1,0:T(8,128)}, f32[128,128]{1,0:T(8,128)}) async-done(((f32[256,1024]{1,0:T(8,128)}, f32[128,128]{1,0:T(8,128)}), (f32[256,1024]{1,0:T(8,128)}, f32[128,128]{1,0:T(8,128)})) %all-reduce.15.cloned.1.call-update) | async-done | bytes 1114128 | tf_op jit(solution)/shard_map/psum | solution.py:42
  798.4 1.0 fusion.41
  799.4 1.6 fusion.16
  801.0 1.6 fusion.26
  802.7 0.2 convolution_negate_fusion.2
  802.9 1.6 convolution_add_fusion.2
  804.5 19.8 %convolution_subtract_fusion.2 = f32[4096,1024]{1,0:T(8,128)} fusion(f32[4096,1024]{1,0:T(8,128)} %convolution_subtract_fusion.3, f32[4096,256]{1,0:T(8,128)} %constant_dynamic-update-slice_fusion.2, f32[128,1024]{1,0:T(8,128)S(1)} %fusion.26, f32[128,1024]{1,0:T(8,128)S(1)} %convolution_add_fusion.2), kind=kOutput, calls=%fused_computation.2 | convolution fusion | flops 12889358336 | bytes 38797312 | tf_op jit(solution)/shard_map/dot_general | solution.py:23
  824.3 18.2 %fusion.42 = f32[256,1024]{1,0:T(8,128)} fusion(f32[4096,256]{1,0:T(8,128)} %constant_dynamic-update-slice_fusion.4, f32[4096,1024]{1,0:T(8,128)} %convolution_subtract_fusion.2), kind=kOutput, calls=%fused_computation.78 | convolution fusion | flops 12884901888 | bytes 22020096 | tf_op jit(solution)/shard_map/dot_general | solution.py:13
  842.4 0.0 all-reduce.13.cloned.1.call-update
  842.5 0.3 all-reduce.11.cloned.1.call-start
  842.7 5.7 fusion.46
  848.4 1.5 constant_dynamic-update-slice_fusion.6
  850.0 49.0 %all-reduce.13.cloned.1.call-done = (f32[256,1024]{1,0:T(8,128)}, f32[128,128]{1,0:T(8,128)}) async-done(((f32[256,1024]{1,0:T(8,128)}, f32[128,128]{1,0:T(8,128)}), (f32[256,1024]{1,0:T(8,128)}, f32[128,128]{1,0:T(8,128)})) %all-reduce.13.cloned.1.call-update) | async-done | bytes 1114128 | tf_op jit(solution)/shard_map/psum | solution.py:42
  899.0 1.0 fusion.44
  900.0 1.6 fusion.14
  901.7 0.0 copy-done.12
  901.7 1.6 fusion.23
  903.3 0.2 convolution_negate_fusion.1
  903.5 1.6 convolution_add_fusion.1
  905.1 19.8 %convolution_subtract_fusion.1 = f32[4096,1024]{1,0:T(8,128)} fusion(f32[4096,1024]{1,0:T(8,128)} %convolution_subtract_fusion.2, f32[4096,256]{1,0:T(8,128)} %constant_dynamic-update-slice_fusion.4, f32[128,1024]{1,0:T(8,128)S(1)} %fusion.23, f32[128,1024]{1,0:T(8,128)S(1)} %convolution_add_fusion.1), kind=kOutput, calls=%fused_computation.1 | convolution fusion | flops 12889358336 | bytes 38797312 | tf_op jit(solution)/shard_map/dot_general | solution.py:23
  925.0 18.0 %fusion.45 = f32[256,1024]{1,0:T(8,128)} fusion(f32[4096,256]{1,0:T(8,128)} %constant_dynamic-update-slice_fusion.6, f32[4096,1024]{1,0:T(8,128)} %convolution_subtract_fusion.1), kind=kOutput, calls=%fused_computation.81 | convolution fusion | flops 12884901888 | bytes 22020096 | tf_op jit(solution)/shard_map/dot_general | solution.py:13
  943.0 0.0 all-reduce.11.cloned.1.call-update
  943.0 56.5 %all-reduce.11.cloned.1.call-done = (f32[256,1024]{1,0:T(8,128)}, f32[128,128]{1,0:T(8,128)}) async-done(((f32[256,1024]{1,0:T(8,128)}, f32[128,128]{1,0:T(8,128)}), (f32[256,1024]{1,0:T(8,128)}, f32[128,128]{1,0:T(8,128)})) %all-reduce.11.cloned.1.call-update) | async-done | bytes 1114128 | tf_op jit(solution)/shard_map/psum | solution.py:42
  999.6 1.0 fusion.47
  1000.6 1.6 fusion.12
  1002.3 1.6 fusion.20
  1003.9 0.2 convolution_negate_fusion
  1004.1 1.6 convolution_add_fusion
  1005.7 19.9 %convolution_subtract_fusion = f32[4096,1024]{1,0:T(8,128)} fusion(f32[4096,1024]{1,0:T(8,128)} %convolution_subtract_fusion.1, f32[4096,256]{1,0:T(8,128)} %constant_dynamic-update-slice_fusion.6, f32[128,1024]{1,0:T(8,128)S(1)} %fusion.20, f32[128,1024]{1,0:T(8,128)S(1)} %convolution_add_fusion), kind=kOutput, calls=%fused_computation | convolution fusion | flops 12889358336 | bytes 38797312 | tf_op jit(solution)/shard_map/dot_general | solution.py:23
  (29 shorter events, 0.1 us)
Async XLA Ops:
  6.5 591.9 %all-reduce.19.cloned.1.call-start = ((), (), s32[]{:S(2)}) async-start(), calls=%async_computation.4 | async-start | bytes 34603008 | tf_op jit(solution)/shard_map/psum | solution.py:9
  16.4 682.1 %all-reduce.17.cloned.1.call-start = ((), (), s32[]{:S(2)}) async-start(), calls=%async_computation.3 | async-start | bytes 2228224 | tf_op jit(solution)/shard_map/psum | solution.py:42
  598.5 2.2 copy-start.8
  598.5 2.9 copy-start.9
  598.5 7.1 copy-start.3
  601.3 5.8 copy-start.5
  605.6 3.1 copy-start.7
  610.3 2.0 copy-start
  612.4 30.4 %copy-start.6 = (f32[4096,128]{1,0:T(8,128)S(1)}, f32[4096,128]{1,0:T(8,128)}, u32[]{:S(2)}) copy-start(f32[4096,128]{1,0:T(8,128)} %get-tuple-element.18) | copy-start | bytes 6291460
  642.5 155.8 %all-reduce.15.cloned.1.call-start = ((), (), s32[]{:S(2)}) async-start(), calls=%async_computation.2 | async-start | bytes 2228224 | tf_op jit(solution)/shard_map/psum | solution.py:42
  642.8 55.7 %copy-start.17 = (f32[128,128]{1,0:T(8,128)S(1)}, f32[128,128]{1,0:T(8,128)}, u32[]{:S(2)}) copy-start(f32[128,128]{1,0:T(8,128)} %get-tuple-element.16) | copy-start | bytes 196612
  642.8 58.6 %copy-start.16 = (f32[128,128]{1,0:T(8,128)S(1)}, f32[128,128]{1,0:T(8,128)}, u32[]{:S(2)}) copy-start(f32[128,128]{1,0:T(8,128)} %get-tuple-element.15) | copy-start | bytes 196612
  698.5 6.4 copy-start.1
  723.7 18.7 %copy-start.4 = (f32[4096,128]{1,0:T(8,128)S(1)}, f32[4096,128]{1,0:T(8,128)}, u32[]{:S(2)}) copy-start(f32[4096,128]{1,0:T(8,128)} %get-tuple-element.22) | copy-start | bytes 6291460
  741.8 157.1 %all-reduce.13.cloned.1.call-start = ((), (), s32[]{:S(2)}) async-start(), calls=%async_computation.1 | async-start | bytes 2228224 | tf_op jit(solution)/shard_map/psum | solution.py:42
  742.4 56.0 %copy-start.15 = (f32[128,128]{1,0:T(8,128)S(1)}, f32[128,128]{1,0:T(8,128)}, u32[]{:S(2)}) copy-start(f32[128,128]{1,0:T(8,128)} %get-tuple-element.20) | copy-start | bytes 196612
  742.4 58.7 %copy-start.14 = (f32[128,128]{1,0:T(8,128)S(1)}, f32[128,128]{1,0:T(8,128)}, u32[]{:S(2)}) copy-start(f32[128,128]{1,0:T(8,128)} %get-tuple-element.19) | copy-start | bytes 196612
  824.3 18.4 %copy-start.2 = (f32[4096,128]{1,0:T(8,128)S(1)}, f32[4096,128]{1,0:T(8,128)}, u32[]{:S(2)}) copy-start(f32[4096,128]{1,0:T(8,128)} %get-tuple-element.26) | copy-start | bytes 6291460
  842.5 157.1 %all-reduce.11.cloned.1.call-start = ((), (), s32[]{:S(2)}) async-start(), calls=%async_computation | async-start | bytes 2228224 | tf_op jit(solution)/shard_map/psum | solution.py:42
  842.7 56.3 %copy-start.13 = (f32[128,128]{1,0:T(8,128)S(1)}, f32[128,128]{1,0:T(8,128)}, u32[]{:S(2)}) copy-start(f32[128,128]{1,0:T(8,128)} %get-tuple-element.24) | copy-start | bytes 196612
  842.7 58.9 %copy-start.12 = (f32[128,128]{1,0:T(8,128)S(1)}, f32[128,128]{1,0:T(8,128)}, u32[]{:S(2)}) copy-start(f32[128,128]{1,0:T(8,128)} %get-tuple-element.23) | copy-start | bytes 196612
  925.0 74.6 %copy-start.11 = (f32[128,128]{1,0:T(8,128)S(1)}, f32[128,128]{1,0:T(8,128)}, u32[]{:S(2)}) copy-start(f32[128,128]{1,0:T(8,128)} %get-tuple-element.28) | copy-start | bytes 196612
  925.0 77.3 %copy-start.10 = (f32[128,128]{1,0:T(8,128)S(1)}, f32[128,128]{1,0:T(8,128)}, u32[]{:S(2)}) copy-start(f32[128,128]{1,0:T(8,128)} %get-tuple-element.27) | copy-start | bytes 196612
Sparse Core Ops, SparseCore 0:
  16.6 581.8 all-reduce.18
  642.6 55.8 all-reduce.16
  742.0 56.3 all-reduce.14
  842.6 56.3 all-reduce.12
  943.2 56.3 all-reduce.10
where the time goes:
time: 1040 us; the launch traced here: 1030 us
  waiting for transfers between devices  785 us (75%)
  matrix products  209 us (20%)
  local copies, waits for them, and re-layouts  14.2 us (1%)
  between operations  14 us (1%)
    psum x1, waiting for transfers between devices, spread(): return lax.psum(block, axis)  582 us
    psum x4, waiting for transfers between devices, shards(): lax.psum((product_t(joined, block), product_t(basis_a, basis_b)), 'row')  203 us
    dot_general x8, matrix products, product_t(): lax.dot_general(left, right, (((0,), (0,)), ((), ())), precision=lax.Prec...  106 us
    dot_general x24, matrix products, matmul(): jnp.dot(left, right, precision=lax.Precision.HIGHEST, preferred_element_t...  103 us
  transfers between devices with their start and end apart: 5, of which 5 were waited for; matrix products, arithmetic and copies ran while one was open for 2% of the time, Pallas kernels for 0%

commit v1 on v0

--- a/solution.py
+++ b/solution.py
@@ -4,9 +4,13 @@
 from jax.sharding import PartitionSpec as P
 
 
+def fix_columns(load, peer_axis):
+    return lax.all_gather(load, peer_axis).sum(axis=0)
+
+
 def spread(block, axis, owner):
     block = jnp.where(lax.axis_index(axis) == owner, block, jnp.zeros_like(block))
-    return lax.psum(block, axis)
+    return fix_columns(block, axis)
 
 
 def product_t(left, right):

time: 1040 us -> 1570 us (1.51)
  waiting for transfers between devices: 785 us -> 1100 us
  blocking collectives: 0 us -> 149 us
  other arithmetic: 9.88 us -> 47.6 us
  matrix products: 209 us -> 243 us
    all_gather x0 -> x8, waiting for transfers between devices: none -> 929 us  [fix_columns(): return lax.all_gather(load, peer_axis).sum(axis=0)]
    psum x1 -> x0, waiting for transfers between devices: 582 us -> none  [spread(): return lax.psum(block, axis)]
    all_gather x0 -> x8, blocking collectives: none -> 149 us  [fix_columns(): return lax.all_gather(load, peer_axis).sum(axis=0)]
    reduce_sum x0 -> x16, other arithmetic: none -> 39.3 us  [fix_columns(): return lax.all_gather(load, peer_axis).sum(axis=0)]
    dot_general x8, matrix products: 106 us -> 144 us  [product_t(): lax.dot_general(left, right, (((0,), (0,)), ((), ())), precision=lax.Prec...]
    psum x4, waiting for transfers between devices: 203 us -> 170 us  [shards(): lax.psum((product_t(joined, block), product_t(basis_a, basis_b)), 'row')]
  transfers between devices with their start and end apart: 5 -> 12, of which waited for: 5 -> 12; matrix products, arithmetic and copies ran while one was open for 2% -> 13% of each run, Pallas kernels for 0% -> 0%
where the time goes in v1:
time: 1570 us; the launch traced here: 1560 us
  waiting for transfers between devices  1100 us (70%)
  matrix products  243 us (15%)
  blocking collectives  149 us (9%)
  other arithmetic  47.6 us (3%)
    all_gather x8, waiting for transfers between devices, fix_columns(): return lax.all_gather(load, peer_axis).sum(axis=0)  929 us
    psum x4, waiting for transfers between devices, shards(): lax.psum((product_t(joined, block), product_t(basis_a, basis_b)), 'row')  170 us
    all_gather x8, blocking collectives, fix_columns(): return lax.all_gather(load, peer_axis).sum(axis=0)  149 us
    dot_general x8, matrix products, product_t(): lax.dot_general(left, right, (((0,), (0,)), ((), ())), precision=lax.Prec...  144 us
    dot_general x24, matrix products, matmul(): jnp.dot(left, right, precision=lax.Precision.HIGHEST, preferred_element_t...  99 us
    reduce_sum x16, other arithmetic, fix_columns(): return lax.all_gather(load, peer_axis).sum(axis=0)  39.3 us
  transfers between devices with their start and end apart: 12, of which 12 were waited for; matrix products, arithmetic and copies ran while one was open for 13% of the time, Pallas kernels for 0%

profile of v1, /device:TPU:0, one launch (start us, length us, event | category | flops | bytes accessed | tf_op | source)
XLA Modules:
  0.0 1557.9 jit_solution(8890528235720694656)
XLA Ops:
  6.5 8.2 slice_select_fusion.4
  14.8 0.7 all-gather.9.cloned.1.call-update
  15.6 0.7 all-gather.13.cloned.1.call-update
  16.3 0.5 all-gather.15.cloned.1.call-update
  16.9 150.4 %all-gather.11.cloned.1.call-done = f32[4,4096,128]{2,1,0:T(8,128)} async-done(((f32[1,4096,128]{2,1,0:T(8,128)}), f32[4,4096,128]{2,1,0:T(8,128)}) %all-gather.11.cloned.1.call-update) | async-done | bytes 8388624 | tf_op jit(solution)/shard_map/all_gather | solution.py:8
  167.3 4.1 reduce_sum.145
  171.4 145.3 %all-gather.9.cloned.1.call-done = f32[4,4096,128]{2,1,0:T(8,128)} async-done(((f32[1,4096,128]{2,1,0:T(8,128)}), f32[4,4096,128]{2,1,0:T(8,128)}) %all-gather.9.cloned.1.call-update) | async-done | bytes 8388624 | tf_op jit(solution)/shard_map/all_gather | solution.py:8
  316.7 5.4 reduce_sum.144
  322.1 6.1 fusion.44
  328.2 30.4 %fusion.3 = f32[256,1024]{1,0:T(8,128)} fusion(f32[4096,1024]{1,0:T(8,128)} %param.3, f32[4096,128]{1,0:T(8,128)S(1)} %reduce_sum.145, f32[4096,128]{1,0:T(8,128)S(1)} %copy-done.4), kind=kOutput, calls=%fused_computation.11 | convolution fusion | flops 12885950464 | bytes 22020096 | tf_op jit(solution)/shard_map/dot_general | solution.py:17
  358.6 0.5 all-gather.17.cloned.1.call-update
  359.2 0.7 all-gather.19.cloned.1.call-update
  360.4 21.6 %all_gather.67 = f32[4,128,128]{2,1,0:T(8,128)S(1)} all-gather(f32[1,128,128]{2,1,0:T(8,128)S(1)} %get-tuple-element.27), channel_id=1, replica_groups=mesh['row'=8,'col'=4] {'col'}, dimensions={0}, use_global_device_ids=true | all-gather | bytes 327680 | tf_op jit(solution)/shard_map/all_gather | solution.py:8
  382.0 19.6 %all_gather.66 = f32[4,128,128]{2,1,0:T(8,128)S(1)} all-gather(f32[1,128,128]{2,1,0:T(8,128)S(1)} %get-tuple-element.28), channel_id=1, replica_groups=mesh['row'=8,'col'=4] {'col'}, dimensions={0}, use_global_device_ids=true | all-gather | bytes 327680 | tf_op jit(solution)/shard_map/all_gather | solution.py:8
  401.7 72.7 %all-gather.13.cloned.1.call-done = f32[4,4096,128]{2,1,0:T(8,128)} async-done(((f32[1,4096,128]{2,1,0:T(8,128)}), f32[4,4096,128]{2,1,0:T(8,128)}) %all-gather.13.cloned.1.call-update) | async-done | bytes 8388624 | tf_op jit(solution)/shard_map/all_gather | solution.py:8
  474.4 4.1 reduce_sum.148
  478.5 145.2 %all-gather.15.cloned.1.call-done = f32[4,4096,128]{2,1,0:T(8,128)} async-done(((f32[1,4096,128]{2,1,0:T(8,128)}), f32[4,4096,128]{2,1,0:T(8,128)}) %all-gather.15.cloned.1.call-update) | async-done | bytes 8388624 | tf_op jit(solution)/shard_map/all_gather | solution.py:8
  623.7 5.4 reduce_sum.149
  629.1 5.8 fusion.46
  634.9 47.2 %all-reduce.15.cloned.1.call-done = (f32[256,1024]{1,0:T(8,128)}, f32[128,128]{1,0:T(8,128)}) async-done(((f32[256,1024]{1,0:T(8,128)}, f32[128,128]{1,0:T(8,128)}), (f32[256,1024]{1,0:T(8,128)}, f32[128,128]{1,0:T(8,128)})) %all-reduce.15.cloned.1.call-update) | async-done | bytes 1114128 | tf_op jit(solution)/shard_map/psum | solution.py:46
  682.1 1.2 fusion.45
  683.5 1.6 fusion.33
  685.1 1.6 fusion.22
  686.8 1.6 convolution_add_fusion.3
  688.4 19.4 %convolution_subtract_fusion.3 = f32[4096,1024]{1,0:T(8,128)} fusion(f32[4096,1024]{1,0:T(8,128)} %param.3, f32[4096,128]{1,0:T(8,128)S(1)} %copy-done.3, f32[4096,128]{1,0:T(8,128)S(1)} %copy-done.5, f32[128,1024]{1,0:T(8,128)S(1)} %fusion.33, f32[128,1024]{1,0:T(8,128)S(1)} %convolution_add_fusion.3), kind=kOutput, calls=%fused_computation.3 | convolution fusion | flops 12890406912 | bytes 38797312 | tf_op jit(solution)/shard_map/dot_general | solution.py:27
  707.8 30.0 %fusion.2 = f32[256,1024]{1,0:T(8,128)} fusion(f32[4096,1024]{1,0:T(8,128)} %convolution_subtract_fusion.3, f32[4096,128]{1,0:T(8,128)S(1)} %copy-done, f32[4096,128]{1,0:T(8,128)S(1)} %reduce_sum.148), kind=kOutput, calls=%fused_computation.10 | convolution fusion | flops 12885950464 | bytes 22020096 | tf_op jit(solution)/shard_map/dot_general | solution.py:17
  737.9 0.7 all-gather.21.cloned.1.call-update
  738.7 0.5 all-gather.23.cloned.1.call-update
  739.3 19.6 %all_gather.70 = f32[4,128,128]{2,1,0:T(8,128)S(1)} all-gather(f32[1,128,128]{2,1,0:T(8,128)S(1)} %get-tuple-element.22), channel_id=1, replica_groups=mesh['row'=8,'col'=4] {'col'}, dimensions={0}, use_global_device_ids=true | all-gather | bytes 327680 | tf_op jit(solution)/shard_map/all_gather | solution.py:8
  758.9 19.1 %all_gather.71 = f32[4,128,128]{2,1,0:T(8,128)S(1)} all-gather(f32[1,128,128]{2,1,0:T(8,128)S(1)} %get-tuple-element.24), channel_id=1, replica_groups=mesh['row'=8,'col'=4] {'col'}, dimensions={0}, use_global_device_ids=true | all-gather | bytes 327680 | tf_op jit(solution)/shard_map/all_gather | solution.py:8
  778.0 62.7 %all-gather.17.cloned.1.call-done = f32[4,4096,128]{2,1,0:T(8,128)} async-done(((f32[1,4096,128]{2,1,0:T(8,128)}), f32[4,4096,128]{2,1,0:T(8,128)}) %all-gather.17.cloned.1.call-update) | async-done | bytes 8388624 | tf_op jit(solution)/shard_map/all_gather | solution.py:8
  840.7 5.4 reduce_sum.152
  846.1 144.0 %all-gather.19.cloned.1.call-done = f32[4,4096,128]{2,1,0:T(8,128)} async-done(((f32[1,4096,128]{2,1,0:T(8,128)}), f32[4,4096,128]{2,1,0:T(8,128)}) %all-gather.19.cloned.1.call-update) | async-done | bytes 8388624 | tf_op jit(solution)/shard_map/all_gather | solution.py:8
  990.2 5.4 reduce_sum.153
  995.5 6.5 fusion.48
  1002.0 46.7 %all-reduce.13.cloned.1.call-done = (f32[256,1024]{1,0:T(8,128)}, f32[128,128]{1,0:T(8,128)}) async-done(((f32[256,1024]{1,0:T(8,128)}, f32[128,128]{1,0:T(8,128)}), (f32[256,1024]{1,0:T(8,128)}, f32[128,128]{1,0:T(8,128)})) %all-reduce.13.cloned.1.call-update) | async-done | bytes 1114128 | tf_op jit(solution)/shard_map/psum | solution.py:46
  1048.7 1.2 fusion.47
  1050.1 1.6 fusion.30
  1051.8 1.6 fusion.20
  1053.4 0.6 convolution_add_fusion.2
  1054.0 19.3 %convolution_subtract_fusion.2 = f32[4096,1024]{1,0:T(8,128)} fusion(f32[4096,1024]{1,0:T(8,128)} %convolution_subtract_fusion.3, f32[4096,128]{1,0:T(8,128)S(1)} %copy-done.1, f32[4096,128]{1,0:T(8,128)S(1)} %reduce_sum.148, f32[128,1024]{1,0:T(8,128)S(1)} %fusion.30, f32[128,1024]{1,0:T(8,128)S(1)} %convolution_add_fusion.2), kind=kOutput, calls=%fused_computation.2 | convolution fusion | flops 12890406912 | bytes 38797312 | tf_op jit(solution)/shard_map/dot_general | solution.py:27
  1073.3 30.0 %fusion.1 = f32[256,1024]{1,0:T(8,128)} fusion(f32[4096,1024]{1,0:T(8,128)} %convolution_subtract_fusion.2, f32[4096,128]{1,0:T(8,128)S(1)} %copy-done.8, f32[4096,128]{1,0:T(8,128)S(1)} %copy-done.6), kind=kOutput, calls=%fused_computation.9 | convolution fusion | flops 12885950464 | bytes 22020096 | tf_op jit(solution)/shard_map/dot_general | solution.py:17
  1103.4 21.9 %all_gather.74 = f32[4,128,128]{2,1,0:T(8,128)S(1)} all-gather(f32[1,128,128]{2,1,0:T(8,128)S(1)} %get-tuple-element.23), channel_id=1, replica_groups=mesh['row'=8,'col'=4] {'col'}, dimensions={0}, use_global_device_ids=true | all-gather | bytes 327680 | tf_op jit(solution)/shard_map/all_gather | solution.py:8
  1125.3 19.0 %all_gather.75 = f32[4,128,128]{2,1,0:T(8,128)S(1)} all-gather(f32[1,128,128]{2,1,0:T(8,128)S(1)} %get-tuple-element.25), channel_id=1, replica_groups=mesh['row'=8,'col'=4] {'col'}, dimensions={0}, use_global_device_ids=true | all-gather | bytes 327680 | tf_op jit(solution)/shard_map/all_gather | solution.py:8
  1144.3 63.2 %all-gather.21.cloned.1.call-done = f32[4,4096,128]{2,1,0:T(8,128)} async-done(((f32[1,4096,128]{2,1,0:T(8,128)}), f32[4,4096,128]{2,1,0:T(8,128)}) %all-gather.21.cloned.1.call-update) | async-done | bytes 8388624 | tf_op jit(solution)/shard_map/all_gather | solution.py:8
  1207.5 4.1 reduce_sum.156
  1211.6 145.2 %all-gather.23.cloned.1.call-done = f32[4,4096,128]{2,1,0:T(8,128)} async-done(((f32[1,4096,128]{2,1,0:T(8,128)}), f32[4,4096,128]{2,1,0:T(8,128)}) %all-gather.23.cloned.1.call-update) | async-done | bytes 8388624 | tf_op jit(solution)/shard_map/all_gather | solution.py:8
  1356.8 5.4 reduce_sum.157
  1362.2 5.7 fusion.50
  1367.9 47.5 %all-reduce.11.cloned.1.call-done = (f32[256,1024]{1,0:T(8,128)}, f32[128,128]{1,0:T(8,128)}) async-done(((f32[256,1024]{1,0:T(8,128)}, f32[128,128]{1,0:T(8,128)}), (f32[256,1024]{1,0:T(8,128)}, f32[128,128]{1,0:T(8,128)})) %all-reduce.11.cloned.1.call-update) | async-done | bytes 1114128 | tf_op jit(solution)/shard_map/psum | solution.py:46
  1415.4 1.2 fusion.49
  1416.5 1.7 fusion.18
  1418.3 1.6 fusion.27
  1420.1 1.6 convolution_add_fusion.1
  1421.8 18.8 %convolution_subtract_fusion.1 = f32[4096,1024]{1,0:T(8,128)} fusion(f32[4096,1024]{1,0:T(8,128)} %convolution_subtract_fusion.2, f32[4096,128]{1,0:T(8,128)S(1)} %copy-done.9, f32[4096,128]{1,0:T(8,128)S(1)} %copy-done.7, f32[128,1024]{1,0:T(8,128)S(1)} %fusion.27, f32[128,1024]{1,0:T(8,128)S(1)} %convolution_add_fusion.1), kind=kOutput, calls=%fused_computation.1 | convolution fusion | flops 12890406912 | bytes 38797312 | tf_op jit(solution)/shard_map/dot_general | solution.py:27
  1440.5 30.0 %fusion = f32[256,1024]{1,0:T(8,128)} fusion(f32[4096,1024]{1,0:T(8,128)} %convolution_subtract_fusion.1, f32[4096,128]{1,0:T(8,128)S(1)} %copy-done.10, f32[4096,128]{1,0:T(8,128)S(1)} %reduce_sum.156), kind=kOutput, calls=%fused_computation.8 | convolution fusion | flops 12885950464 | bytes 22020096 | tf_op jit(solution)/shard_map/dot_general | solution.py:17
  1470.6 14.0 all_gather.78
  1484.6 14.2 all_gather.79
  1498.8 28.3 %all-reduce.9.cloned.1.call-done = (f32[256,1024]{1,0:T(8,128)}, f32[128,128]{1,0:T(8,128)}) async-done(((f32[256,1024]{1,0:T(8,128)}, f32[128,128]{1,0:T(8,128)}), (f32[256,1024]{1,0:T(8,128)}, f32[128,128]{1,0:T(8,128)})) %all-reduce.9.cloned.1.call-update) | async-done | bytes 1114128 | tf_op jit(solution)/shard_map/psum | solution.py:46
  1527.1 1.2 fusion.51
  1528.3 1.6 fusion.16
  1529.9 1.6 fusion.24
  1531.8 0.6 convolution_add_fusion
  1532.4 18.5 %convolution_subtract_fusion = f32[4096,1024]{1,0:T(8,128)} fusion(f32[4096,1024]{1,0:T(8,128)} %convolution_subtract_fusion.1, f32[4096,128]{1,0:T(8,128)S(1)} %copy-done.11, f32[4096,128]{1,0:T(8,128)S(1)} %reduce_sum.156, f32[128,1024]{1,0:T(8,128)S(1)} %fusion.24, f32[128,1024]{1,0:T(8,128)S(1)} %convolution_add_fusion), kind=kOutput, calls=%fused_computation | convolution fusion | flops 12890406912 | bytes 38797312 | tf_op jit(solution)/shard_map/dot_general | solution.py:27
  (60 shorter events, 2.0 us)
Async XLA Ops:
  6.5 160.8 %all-gather.11.cloned.1.call-start = ((), (), s32[]{:S(2)}) async-start(), calls=%async_computation.1 | async-start | bytes 10485760 | tf_op jit(solution)/shard_map/all_gather | solution.py:8
  14.8 301.9 %all-gather.9.cloned.1.call-start = ((), (), s32[]{:S(2)}) async-start(), calls=%async_computation | async-start | bytes 10485760 | tf_op jit(solution)/shard_map/all_gather | solution.py:8
  15.6 458.9 %all-gather.13.cloned.1.call-start = ((), (), s32[]{:S(2)}) async-start(), calls=%async_computation.2 | async-start | bytes 10485760 | tf_op jit(solution)/shard_map/all_gather | solution.py:8
  16.3 607.4 %all-gather.15.cloned.1.call-start = ((), (), s32[]{:S(2)}) async-start(), calls=%async_computation.3 | async-start | bytes 10485760 | tf_op jit(solution)/shard_map/all_gather | solution.py:8
  16.9 665.2 %all-reduce.15.cloned.1.call-start = ((), (), s32[]{:S(2)}) async-start(), calls=%async_computation.11 | async-start | bytes 2228224 | tf_op jit(solution)/shard_map/psum | solution.py:46
  171.4 156.8 %copy-start.2 = (f32[4096,128]{1,0:T(8,128)}, f32[4096,128]{1,0:T(8,128)S(1)}, u32[]{:S(2)}) copy-start(f32[4096,128]{1,0:T(8,128)S(1)} %reduce_sum.145) | copy-start | bytes 6291460
  322.1 6.1 copy-start.4
  358.5 482.2 %all-gather.17.cloned.1.call-start = ((), (), s32[]{:S(2)}) async-start(), calls=%async_computation.4 | async-start | bytes 10485760 | tf_op jit(solution)/shard_map/all_gather | solution.py:8
  358.6 1.8 copy-start.14
  359.1 631.0 %all-gather.19.cloned.1.call-start = ((), (), s32[]{:S(2)}) async-start(), calls=%async_computation.5 | async-start | bytes 10485760 | tf_op jit(solution)/shard_map/all_gather | solution.py:8
  359.9 688.8 %all-reduce.13.cloned.1.call-start = ((), (), s32[]{:S(2)}) async-start(), calls=%async_computation.10 | async-start | bytes 2228224 | tf_op jit(solution)/shard_map/psum | solution.py:46
  682.1 6.3 copy-start.3
  682.1 6.3 copy-start.5
  688.4 19.5 %copy-start = (f32[4096,128]{1,0:T(8,128)S(1)}, f32[4096,128]{1,0:T(8,128)}, u32[]{:S(2)}) copy-start(f32[4096,128]{1,0:T(8,128)} %reduce_sum.149) | copy-start | bytes 6291460
  737.9 469.6 %all-gather.21.cloned.1.call-start = ((), (), s32[]{:S(2)}) async-start(), calls=%async_computation.6 | async-start | bytes 10485760 | tf_op jit(solution)/shard_map/all_gather | solution.py:8
  738.6 618.1 %all-gather.23.cloned.1.call-start = ((), (), s32[]{:S(2)}) async-start(), calls=%async_computation.7 | async-start | bytes 10485760 | tf_op jit(solution)/shard_map/all_gather | solution.py:8
  739.2 676.1 %all-reduce.11.cloned.1.call-start = ((), (), s32[]{:S(2)}) async-start(), calls=%async_computation.9 | async-start | bytes 2228224 | tf_op jit(solution)/shard_map/psum | solution.py:46
  1048.7 4.7 copy-start.12
  1048.7 5.3 copy-start.1
  1054.0 19.3 %copy-start.6 = (f32[4096,128]{1,0:T(8,128)S(1)}, f32[4096,128]{1,0:T(8,128)}, u32[]{:S(2)}) copy-start(f32[4096,128]{1,0:T(8,128)} %reduce_sum.152) | copy-start | bytes 6291460
  1054.0 19.3 %copy-start.8 = (f32[4096,128]{1,0:T(8,128)S(1)}, f32[4096,128]{1,0:T(8,128)}, u32[]{:S(2)}) copy-start(f32[4096,128]{1,0:T(8,128)} %reduce_sum.153) | copy-start | bytes 6291460
  1103.3 423.8 %all-reduce.9.cloned.1.call-start = ((), (), s32[]{:S(2)}) async-start(), calls=%async_computation.8 | async-start | bytes 2228224 | tf_op jit(solution)/shard_map/psum | solution.py:46
  1415.3 6.4 copy-start.7
  1415.4 6.4 copy-start.9
  1421.7 18.8 %copy-start.10 = (f32[4096,128]{1,0:T(8,128)S(1)}, f32[4096,128]{1,0:T(8,128)}, u32[]{:S(2)}) copy-start(f32[4096,128]{1,0:T(8,128)} %reduce_sum.157) | copy-start | bytes 6291460
  1527.1 4.7 copy-start.13
  1527.1 5.3 copy-start.11
Sparse Core Ops, SparseCore 0:
  14.9 152.3 all-gather.10
  168.9 147.7 all-gather.8
  318.3 156.1 all-gather.12
  475.8 147.8 all-gather.14
  626.8 55.2 all-reduce.14
  683.5 157.1 all-gather.16
  842.3 147.8 all-gather.18
  993.4 55.2 all-reduce.12
  1050.3 157.1 all-gather.20
  1208.9 147.8 all-gather.22
  1360.0 55.2 all-reduce.10
  1470.7 56.3 all-reduce.8
